TPU v7x, 256 devices: a whole 4x4x8 slice. The times are simulated.
256 devices in a mesh: zero: 32 (over y, x, core), tp: 8 (over z).
Axes of the slice: x: 4, y: 4, z: 8, core: 2. Of those that a mesh axis runs over, the one named last changes fastest.
Arguments:
- weight_gate: bfloat16 [2560, 9728], P('zero', 'tp'), may hold values from -0.125 to 0.125
- low_gate: bfloat16 [2560, 16], P('zero'), may hold values from -0.125 to 0.125
- high_gate: bfloat16 [16, 9728], P(None, 'tp'), may hold values from -1.5 to 1.5
- weight_up: bfloat16 [2560, 9728], P('zero', 'tp'), may hold values from -0.125 to 0.125
- low_up: bfloat16 [2560, 16], P('zero'), may hold values from -0.125 to 0.125
- high_up: bfloat16 [16, 9728], P(None, 'tp'), may hold values from -1.5 to 1.5
- weight_down: bfloat16 [9728, 2560], P('tp', 'zero'), may hold values from -0.0625 to 0.0625
- low_down: bfloat16 [9728, 16], P('tp'), may hold values from -0.0625 to 0.0625
- high_down: bfloat16 [16, 2560], P(None, 'zero'), may hold values from -1.5 to 1.5
- norm_train: float32 [2560], P(('zero', 'tp')), may hold values from 0.25 to 1.75
- norm_step: float32 [2560], P(('zero', 'tp')), may hold values from -0.3 to 0.3
Outputs:
- ready_gate: bfloat16 [2560, 9728], P(None, 'tp')
- ready_up: bfloat16 [2560, 9728], P(None, 'tp')
- ready_down: bfloat16 [9728, 2560], P('tp')
- serve_norm: bfloat16 [2560], replicated
All inputs are finite; a program needn't handle non-finite values.
Results may differ from a plain program's by a relative error of at most 0.001.
Values may be sent and summed in bfloat16 or wider, within the bound.
No kernel may reach another device: no remote copies, remote signals or barrier semaphores. Data moves between devices by JAX's collectives and lax.ppermute only.
A program may use at most 128 MiB of HBM per device.

v0:
```python
import jax
import jax.numpy as jnp
from jax import lax
from jax.sharding import Mesh
from jax.sharding import PartitionSpec as P

ZERO = ("zero_0", "zero_1", "zero_2")
ZERO_TP = ("zero_0", "zero_1", "zero_2", "tp")
mix_rate = 0.5


def turned_gather(arrays, axis, dims):
    turned = [jnp.moveaxis(a, dim, 0) for a, dim in zip(arrays, dims)]
    widths = [t[0].size for t in turned]
    both = jnp.concatenate([t.reshape(-1, w) for t, w in zip(turned, widths)], axis=1)
    out = lax.all_gather(both, axis, axis=0, tiled=True)
    pieces = jnp.split(out, [sum(widths[:k]) for k in range(1, len(widths))], axis=1)
    return tuple(
        (
            jnp.moveaxis(b.reshape(-1, *t.shape[1:]), 0, dim)
            for b, t, dim in zip(pieces, turned, dims)
        )
    )


def laid_out(pieces, dim):
    pieces = jnp.moveaxis(pieces, 0, dim)
    dims = pieces.shape
    return pieces.reshape(*dims[:dim], dims[dim] * dims[dim + 1], *dims[dim + 2 :])


def all_blocks(value, axes, turns):
    pieces = value
    for k in turns:
        pieces = lax.all_gather(pieces, axes[k])
    done = turns[::-1]
    back = [done.index(k) for k in range(len(axes))]
    pieces = pieces.transpose(*back, *range(len(axes), pieces.ndim))
    return pieces.reshape(-1, *value.shape)


def gathered_by_axis(value, axes, turns, dim):
    return laid_out(all_blocks(value, axes, turns), dim)


def local(
    weight_gate,
    low_gate,
    high_gate,
    weight_up,
    low_up,
    high_up,
    weight_down,
    low_down,
    high_down,
    norm_train,
    norm_step,
):
    latest_gate = weight_gate.astype(jnp.float32) + mix_rate * jnp.dot(
        low_gate, high_gate, preferred_element_type=jnp.float32
    )
    latest_up = weight_up.astype(jnp.float32) + mix_rate * jnp.dot(
        low_up, high_up, preferred_element_type=jnp.float32
    )
    latest_down = weight_down.astype(jnp.float32) + mix_rate * jnp.dot(
        low_down, high_down, preferred_element_type=jnp.float32
    )
    narrow_gate, narrow_up, narrow_down = (
        latest_gate.astype(jnp.bfloat16),
        latest_up.astype(jnp.bfloat16),
        latest_down.astype(jnp.bfloat16),
    )
    ready_gate, ready_up, ready_down = turned_gather(
        (narrow_gate, narrow_up, narrow_down), ZERO, (0, 0, 1)
    )
    serve_norm = gathered_by_axis(
        (norm_train + norm_step).astype(jnp.bfloat16), ZERO_TP, (0, 1, 3, 2), 0
    )
    return (ready_gate, ready_up, ready_down, serve_norm)


def solution(mesh):
    finer = Mesh(
        mesh.devices.reshape(4, 4, 2, mesh.shape["tp"]), ("zero_0", "zero_1", "zero_2", "tp")
    )
    return jax.shard_map(
        local,
        mesh=finer,
        in_specs=(
            P(ZERO, "tp"),
            P(ZERO, None),
            P(None, "tp"),
            P(ZERO, "tp"),
            P(ZERO, None),
            P(None, "tp"),
            P("tp", ZERO),
            P("tp", None),
            P(None, ZERO),
            P(ZERO_TP),
            P(ZERO_TP),
        ),
        out_specs=(P(None, "tp"), P(None, "tp"), P("tp", None), P()),
        check_vma=False,
    )
```

profile of v0, /device:TPU:1, one launch (start us, length us, event | category | flops | bytes accessed | tf_op | source)
XLA Modules:
  0.0 150.4 jit_solution(1845330764220144492)
XLA Ops:
  7.2 0.0 copy-start
  7.2 0.0 all-gather.7.cloned.1.call-start
  7.2 0.7 copy-done
  8.0 1.2 fusion.3
  9.1 1.2 fusion.4
  10.4 1.2 fusion.6
  11.6 1.1 concatenate.3
  12.7 0.0 all-gather.7.cloned.1.call-update
  12.7 1.3 dynamic-slice
  14.6 0.7 add_convert_fusion
  15.3 0.2 dynamic-update-slice
  15.5 9.5 %all-reduce = bf16[40]{0:T(256)(128)(2,1)S(1)} all-reduce(bf16[40]{0:T(256)(128)(2,1)S(1)} %dynamic-update-slice), channel_id=2, replica_groups=mesh['zero_0'=4,'zero_1'=4,'zero_2'=2,'tp'=8] {'zero_0'}, use_global_device_ids=true, to_apply=%add | all-reduce | flops 40 | bytes 160
  25.0 0.1 reshape.15
  25.1 7.7 %all-gather.4 = bf16[4,4,10]{2,1,0:T(4,128)(2,1)S(1)} all-gather(bf16[1,4,10]{2,1,0:T(4,128)(2,1)S(1)} %reshape.15), channel_id=3, replica_groups=mesh['zero_0'=4,'zero_1'=4,'zero_2'=2,'tp'=8] {'zero_1'}, dimensions={0}, use_global_device_ids=true | all-gather | bytes 400 | tf_op jit(solution)/shard_map/all_gather | solution.py:35
  32.8 23.2 %all-gather.2 = bf16[32,4,10]{2,1,0:T(4,128)(2,1)S(1)} all-gather(bf16[4,4,10]{2,1,0:T(4,128)(2,1)S(1)} %all-gather.4), channel_id=4, replica_groups=mesh['zero_0'=4,'zero_1'=4,'zero_2'=2,'tp'=8] {'tp'}, dimensions={0}, use_global_device_ids=true | all-gather | bytes 2880 | tf_op jit(solution)/shard_map/all_gather | solution.py:35
  56.0 11.3 %all-gather.3 = bf16[16,4,4,10]{3,2,1,0:T(4,128)(2,1)S(1)} all-gather(bf16[8,4,4,10]{3,2,1,0:T(4,128)(2,1)S(1)} %bitcast.20), channel_id=5, replica_groups=mesh['zero_0'=4,'zero_1'=4,'zero_2'=2,'tp'=8] {'zero_2'}, dimensions={0}, use_global_device_ids=true | all-gather | bytes 7680 | tf_op jit(solution)/shard_map/all_gather | solution.py:35
  67.3 0.7 reshape_reshape.3
  68.1 31.7 %all-gather.7.cloned.1.call-done = bf16[2560,3648]{1,0:T(8,128)(2,1)} async-done(((bf16[80,3648]{1,0:T(8,128)(2,1)}), bf16[2560,3648]{1,0:T(8,128)(2,1)}) %all-gather.7.cloned.1.call-update) | async-done | bytes 18677776 | tf_op jit(solution)/shard_map/all_gather | solution.py:16
  99.7 15.8 %slice_bitcast_fusion = (bf16[1216,2560]{0,1:T(8,128)(2,1)}, bf16[2560,1216]{1,0:T(8,128)(2,1)}, bf16[2560,1216]{1,0:T(8,128)(2,1)}) fusion(bf16[2560,3648]{1,0:T(8,128)(2,1)} %all-gather.7.cloned.1.call-done), kind=kLoop, calls=%fused_computation | loop fusion | bytes 37355520 | tf_op jit(solution)/shard_map/transpose | solution.py:20
  115.5 9.3 %copy.23 = bf16[2560,1216]{0,1:T(8,128)(2,1)} copy(bf16[2560,1216]{1,0:T(8,128)(2,1)} %get-tuple-element.18) | data formatting | bytes 12451840
  124.9 9.3 %copy.24 = bf16[2560,1216]{0,1:T(8,128)(2,1)} copy(bf16[2560,1216]{1,0:T(8,128)(2,1)} %get-tuple-element.17) | data formatting | bytes 12451840
  134.2 9.3 %copy.25 = bf16[1216,2560]{1,0:T(8,128)(2,1)} copy(bf16[1216,2560]{0,1:T(8,128)(2,1)} %get-tuple-element.16) | data formatting | bytes 12451840
  (2 shorter events, 0.0 us)
Async XLA Ops:
  7.2 0.8 copy-start
  7.2 92.5 %all-gather.7.cloned.1.call-start = ((), (), s32[]{:S(2)}) async-start(), calls=%async_computation | async-start | bytes 19599360 | tf_op jit(solution)/shard_map/all_gather | solution.py:16
Sparse Core Ops, SparseCore 0:
  12.8 86.8 all-gather.6
where the time goes:
time: 151 us; the launch traced here: 150 us
  blocking collectives  51.7 us (34%)
  local copies, waits for them, and re-layouts  47.9 us (32%)
  waiting for transfers between devices  31.7 us (21%)
  between operations  14.7 us (10%)
  matrix products  3.63 us (2%)
    all_gather x3, blocking collectives, all_blocks(): pieces = lax.all_gather(pieces, axes[k])  42.2 us
    all_gather x1, waiting for transfers between devices, turned_gather(): out = lax.all_gather(both, axis, axis=0, tiled=True)  31.7 us
    unnamed x9, local copies, waits for them, and re-layouts  30.3 us
    transpose x1, local copies, waits for them, and re-layouts, turned_gather(): jnp.moveaxis(b.reshape(-1, *t.shape[1:]), 0, dim)  15.8 us
    unnamed x1, blocking collectives  9.52 us
  transfers between devices with their start and end apart: 1, of which 1 were waited for; matrix products, arithmetic and copies ran while one was open for 2% of the time, Pallas kernels for 0%

commit v1 on v0

--- a/solution.py
+++ b/solution.py
@@ -13,7 +13,9 @@
     turned = [jnp.moveaxis(a, dim, 0) for a, dim in zip(arrays, dims)]
     widths = [t[0].size for t in turned]
     both = jnp.concatenate([t.reshape(-1, w) for t, w in zip(turned, widths)], axis=1)
-    out = lax.all_gather(both, axis, axis=0, tiled=True)
+    out = jnp.concatenate(
+        lax.all_to_all(jnp.stack([both] * lax.axis_size(axis)), axis, 0, 0), axis=0
+    )
     pieces = jnp.split(out, [sum(widths[:k]) for k in range(1, len(widths))], axis=1)
     return tuple(
         (

time: 151 us -> 338 us (2.24); the launches traced: 150 us -> 333 us
  blocking collectives: 51.7 us -> 266 us
  waiting for transfers between devices: 31.7 us -> 0.01 us
  between operations: 14.7 us -> 1.38 us
  starting transfers between devices: 0.04 us -> 8.75 us
  local copies, waits for them, and re-layouts: 47.9 us -> 53.3 us
    unnamed x1, blocking collectives: 9.52 us -> 224 us
    all_gather x1 -> x0, waiting for transfers between devices: 31.7 us -> none  [turned_gather(): out = lax.all_gather(both, axis, axis=0, tiled=True)]
    all_to_all x0 -> x1, starting transfers between devices: none -> 8.75 us  [turned_gather(): lax.all_to_all(jnp.stack([both] * lax.axis_size(axis)), axis, 0, 0)]
    another operation x0 -> x1, local copies, waits for them, and re-layouts: none -> 6.66 us  [turned_gather(): jnp.stack([both] * lax.axis_size(axis))]
    unnamed x9 -> x17, local copies, waits for them, and re-layouts: 30.3 us -> 29.7 us
  transfers between devices with their start and end apart: 1 -> 1, of which waited for: 1 -> 0; matrix products, arithmetic and copies ran while one was open for 2% -> 1% of each run, Pallas kernels for 0% -> 0%
where the time goes in v1:
time: 338 us; the launch traced here: 333 us
  blocking collectives  266 us (79%)
  local copies, waits for them, and re-layouts  53.3 us (16%)
  starting transfers between devices  8.75 us (3%)
  matrix products  3.63 us (1%)
    unnamed x1, blocking collectives  224 us
    all_gather x3, blocking collectives, all_blocks(): pieces = lax.all_gather(pieces, axes[k])  41.9 us
    unnamed x17, local copies, waits for them, and re-layouts  29.7 us
    transpose x1, local copies, waits for them, and re-layouts, turned_gather(): jnp.moveaxis(b.reshape(-1, *t.shape[1:]), 0, dim)  15.8 us
    all_to_all x1, starting transfers between devices, turned_gather(): lax.all_to_all(jnp.stack([both] * lax.axis_size(axis)), axis, 0, 0)  8.75 us
  transfers between devices with their start and end apart: 1, of which 0 were waited for; matrix products, arithmetic and copies ran while one was open for 1% of the time, Pallas kernels for 0%

profile of v1, /device:TPU:1, one launch (start us, length us, event | category | flops | bytes accessed | tf_op | source)
XLA Modules:
  0.0 332.9 jit_solution(14690212333028656014)
XLA Ops:
  0.6 0.0 copy-start
  0.6 0.8 copy-done
  1.4 1.2 fusion.3
  2.6 1.2 fusion.4
  3.8 1.2 fusion.6
  5.1 0.4 concatenate.3
  5.4 6.7 %stack.2 = bf16[32,80,3648]{2,1,0:T(8,128)(2,1)} broadcast(bf16[80,3648]{1,0:T(8,128)(2,1)S(1)} %concatenate.3), dimensions={1,2} | broadcast | bytes 19261440 | tf_op jit(solution)/shard_map/stack | solution.py:17
  12.1 0.0 copy-start.4
  12.1 0.0 copy-start.2
  12.1 0.0 copy-start.3
  12.1 8.8 %all-to-all-start = ((bf16[32,80,3648]{2,1,0:T(8,128)(2,1)}), bf16[32,80,3648]{2,1,0:T(8,128)(2,1)}, u32[]{:S(2)}, u32[]{:S(2)}) async-start(bf16[32,80,3648]{2,1,0:T(8,128)(2,1)} %stack.2), calls=%async_computation | async-start | bytes 38010880 | tf_op jit(solution)/shard_map/all_to_all | solution.py:17
  20.9 0.0 copy-done.4
  20.9 0.6 dynamic-slice
  22.1 0.0 copy-done.2
  22.1 0.0 copy-done.3
  22.2 0.2 dynamic-update-slice
  22.4 223.9 %all-reduce = bf16[40]{0:T(256)(128)(2,1)S(1)} all-reduce(bf16[40]{0:T(256)(128)(2,1)S(1)} %dynamic-update-slice), channel_id=2, replica_groups=mesh['zero_0'=4,'zero_1'=4,'zero_2'=2,'tp'=8] {'zero_0'}, use_global_device_ids=true, to_apply=%add | all-reduce | flops 40 | bytes 160
  246.3 0.1 reshape.21
  246.4 10.7 %all-gather.4 = bf16[4,4,10]{2,1,0:T(4,128)(2,1)S(1)} all-gather(bf16[1,4,10]{2,1,0:T(4,128)(2,1)S(1)} %reshape.21), channel_id=3, replica_groups=mesh['zero_0'=4,'zero_1'=4,'zero_2'=2,'tp'=8] {'zero_1'}, dimensions={0}, use_global_device_ids=true | all-gather | bytes 400 | tf_op jit(solution)/shard_map/all_gather | solution.py:37
  257.1 22.0 %all-gather.2 = bf16[32,4,10]{2,1,0:T(4,128)(2,1)S(1)} all-gather(bf16[4,4,10]{2,1,0:T(4,128)(2,1)S(1)} %all-gather.4), channel_id=4, replica_groups=mesh['zero_0'=4,'zero_1'=4,'zero_2'=2,'tp'=8] {'tp'}, dimensions={0}, use_global_device_ids=true | all-gather | bytes 2880 | tf_op jit(solution)/shard_map/all_gather | solution.py:37
  279.1 9.2 %all-gather.3 = bf16[16,4,4,10]{3,2,1,0:T(4,128)(2,1)S(1)} all-gather(bf16[8,4,4,10]{3,2,1,0:T(4,128)(2,1)S(1)} %bitcast.21), channel_id=5, replica_groups=mesh['zero_0'=4,'zero_1'=4,'zero_2'=2,'tp'=8] {'zero_2'}, dimensions={0}, use_global_device_ids=true | all-gather | bytes 7680 | tf_op jit(solution)/shard_map/all_gather | solution.py:37
  288.3 0.7 reshape_reshape.3
  289.1 0.0 all-to-all-done
  289.1 15.8 %slice_bitcast_fusion = (bf16[1216,2560]{0,1:T(8,128)(2,1)}, bf16[2560,1216]{1,0:T(8,128)(2,1)}, bf16[2560,1216]{1,0:T(8,128)(2,1)}) fusion(bf16[2560,3648]{1,0:T(8,128)(2,1)} %bitcast.1), kind=kLoop, calls=%fused_computation | loop fusion | bytes 37355520 | tf_op jit(solution)/shard_map/transpose | solution.py:22
  304.9 9.3 %copy.21 = bf16[2560,1216]{0,1:T(8,128)(2,1)} copy(bf16[2560,1216]{1,0:T(8,128)(2,1)} %get-tuple-element.14) | data formatting | bytes 12451840
  314.2 0.0 copy-start.1
  314.2 9.3 %copy.22 = bf16[2560,1216]{0,1:T(8,128)(2,1)} copy(bf16[2560,1216]{1,0:T(8,128)(2,1)} %get-tuple-element.13) | data formatting | bytes 12451840
  323.6 9.3 %copy.23 = bf16[1216,2560]{1,0:T(8,128)(2,1)} copy(bf16[1216,2560]{0,1:T(8,128)(2,1)} %get-tuple-element.12) | data formatting | bytes 12451840
  332.9 0.0 copy-done.1
  (3 shorter events, 0.0 us)
Async XLA Ops:
  0.6 0.8 copy-start
  12.1 8.8 %copy-start.4 = (u32[256]{0:T(256)S(1)}, u32[256]{0:T(256)}, u32[]{:S(2)}) copy-start(u32[256]{0:T(256)} %constant.13) | copy-start | bytes 3076
  12.1 10.0 %copy-start.2 = (f32[10]{0:T(128)S(1)}, f32[10]{0:T(128)}, u32[]{:S(2)}) copy-start(f32[10]{0:T(128)} %param.20) | copy-start | bytes 124
  12.1 10.0 %copy-start.3 = (f32[10]{0:T(128)S(1)}, f32[10]{0:T(128)}, u32[]{:S(2)}) copy-start(f32[10]{0:T(128)} %param.21) | copy-start | bytes 124
  12.1 277.0 %all-to-all-start = ((bf16[32,80,3648]{2,1,0:T(8,128)(2,1)}), bf16[32,80,3648]{2,1,0:T(8,128)(2,1)}, u32[]{:S(2)}, u32[]{:S(2)}) async-start(bf16[32,80,3648]{2,1,0:T(8,128)(2,1)} %stack.2), calls=%async_computation | async-start | bytes 38010880 | tf_op jit(solution)/shard_map/all_to_all | solution.py:17
  314.2 18.7 %copy-start.1 = (bf16[16,1216]{1,0:T(8,128)(2,1)S(1)}, bf16[16,1216]{1,0:T(8,128)(2,1)}, u32[]{:S(2)}) copy-start(bf16[16,1216]{1,0:T(8,128)(2,1)} %param.13) | copy-start | bytes 116740
